TPU v7x, 16 devices: a whole 2x2x2 slice. The times are simulated.
16 devices in a mesh: fsdp: 16 (over z, y, x, core).
Axes of the slice: x: 2, y: 2, z: 2, core: 2. Of those that a mesh axis runs over, the one named last changes fastest.
Arguments:
- left_mat: bfloat16 [65536, 2048], P('fsdp')
- right_mat: bfloat16 [2048, 2048], P('fsdp')
Outputs:
- output: bfloat16 [65536, 2048], P('fsdp')
All inputs are finite; a program needn't handle non-finite values.
Results may differ from a plain program's by a relative error of at most 0.001.
Values are sent between devices in bfloat16 or wider.
A program may use at most 1 GiB of HBM per device.

v0:
```python
import jax
import jax.numpy as jnp
from jax import lax
from jax.sharding import PartitionSpec as P


def solution(mesh):
    spec_rows = P("fsdp", None)

    def local_fn(left_blk, right_blk):
        full_right = lax.all_gather(right_blk, "fsdp", axis=0, tiled=True)
        return jnp.dot(left_blk, full_right, preferred_element_type=jnp.float32).astype(jnp.bfloat16)

    return jax.shard_map(local_fn, mesh=mesh, in_specs=(spec_rows, spec_rows), out_specs=spec_rows, check_vma=False)
```

profile of v0, /device:TPU:0, one launch (start us, length us, event | category | flops | bytes accessed | tf_op | source)
XLA Modules:
  0.0 109.8 jit_solution(868784670706194940)
XLA Ops:
  6.5 0.0 all-gather.2.cloned.1.call-start
  6.5 0.7 all-gather.2.cloned.1.call-update
  7.3 53.8 %all-gather.2.cloned.1.call-done = bf16[2048,2048]{1,0:T(8,128)(2,1)} async-done(((bf16[128,2048]{1,0:T(8,128)(2,1)}), bf16[2048,2048]{1,0:T(8,128)(2,1)}) %all-gather.2.cloned.1.call-update) | async-done | bytes 8388624 | tf_op jit(solution)/shard_map/all_gather | solution.py:11
  61.1 41.8 %convolution_convert_fusion = bf16[4096,2048]{1,0:T(8,128)(2,1)} fusion(bf16[4096,2048]{1,0:T(8,128)(2,1)} %param.2, bf16[2048,2048]{1,0:T(8,128)(2,1)} %all-gather.2.cloned.1.call-done), kind=kOutput, calls=%fused_computation | convolution fusion | flops 34368126976 | bytes 41943040 | tf_op jit(solution)/shard_map/dot_general | solution.py:12
Async XLA Ops:
  6.5 54.5 %all-gather.2.cloned.1.call-start = ((), (), s32[]{:S(2)}) async-start(), calls=%async_computation | async-start | bytes 8912896 | tf_op jit(solution)/shard_map/all_gather | solution.py:11
Sparse Core Ops, SparseCore 0:
  9.6 51.4 all-gather.1
where the time goes:
time: 110 us
  waiting for transfers between devices  54.5 us (50%)
  matrix products  41.8 us (38%)
  between operations  13.4 us (12%)
    all_gather x1, waiting for transfers between devices, local_fn(): full_right = lax.all_gather(right_blk, 'fsdp', axis=0, tiled=True)  53.8 us
    dot_general x1, matrix products, local_fn(): jnp.dot(left_blk, full_right, preferred_element_type=jnp.float32)  41.8 us
  transfers between devices with their start and end apart: 1, of which 1 were waited for; matrix products, arithmetic and copies ran while one was open for 0% of the time, Pallas kernels for 0%

commit v1 on v0

v1 whole, which is shorter than its diff:
```python
import functools

import jax
import jax.numpy as jnp
from jax import lax
from jax.experimental import pallas as pl
from jax.experimental.pallas import tpu as pltpu
from jax.sharding import PartitionSpec as P

MESH = pl.DeviceIdType.MESH
CHUNKS = 4
SUB = 256
LAST = 512


def flip(index, stride):
    return index + stride - 2 * stride * lax.rem(lax.div(index, stride), 2)


def dot(a, b):
    return jnp.dot(a, b, preferred_element_type=jnp.float32)


def gather_kernel(a_hbm, b_hbm, b_all, a_all, acc, a_sem, own_sem, send_sem, recv_sem, pair_send, pair_recv, far_send, far_recv):
    me = lax.axis_index("fsdp")
    depth = b_hbm.shape[0]
    wide = b_all.shape[2]
    rows = acc.shape[1]
    half = rows // 2
    mate = flip(me, 1)
    dev_x, dev_y, dev_z = flip(me, 2), flip(me, 4), flip(me, 8)
    dev_xy, dev_yz, dev_zx = flip(dev_x, 4), flip(dev_y, 8), flip(dev_z, 2)
    dev_far = flip(dev_xy, 8)
    near = (dev_x, dev_y, dev_z)
    diag = (dev_xy, dev_yz, dev_zx)
    order = (me, *near, *diag, dev_far)

    def chip_rows(device):
        return pl.ds(pl.multiple_of(lax.div(device, 2) * (2 * depth), 2 * depth), 2 * depth)

    def block(j, device, columns=slice(None)):
        return b_all.at[j, pl.ds(pl.multiple_of(device * depth, depth), depth), columns]

    def link(kind, j, device, target):
        ref = block(j, device)
        return pltpu.make_async_remote_copy(ref, ref, send_sem.at[kind, j], recv_sem.at[kind, j], device_id=(target,), device_id_type=MESH)

    def pair(kind, j, device):
        ref = block(j, device)
        return pltpu.make_async_remote_copy(ref, ref, pair_send.at[kind, j], pair_recv.at[kind, j], device_id=(mate,), device_id_type=MESH)

    w4 = wide // 4
    pieces = ((2, 0, slice(None)), (0, 1, slice(None)), (1, 2, slice(None)),
              (2, 3, pl.ds(0, w4)), (0, 3, pl.ds(w4, w4)), (1, 3, pl.ds(2 * w4, 2 * w4)))
    carried = {2: dev_xy, 0: dev_yz, 1: dev_zx}

    def far(p, device):
        d, j, columns = pieces[p]
        ref = block(j, device, columns)
        return pltpu.make_async_remote_copy(ref, ref, far_send.at[p], far_recv.at[p], device_id=(near[d],), device_id_type=MESH)

    def a_copy(i):
        cols = chip_rows(order[i])
        return pltpu.make_async_copy(a_hbm.at[:, cols], a_all.at[:, cols], a_sem.at[i])

    def own_copy(j):
        return pltpu.make_async_copy(b_hbm.at[:, pl.ds(j * wide, wide)], block(j, me), own_sem.at[j])

    for j in range(CHUNKS):
        own_copy(j).start()
    for i in range(8):
        a_copy(i).start()

    barrier = pltpu.get_barrier_semaphore()
    for device in (mate, *near):
        pl.semaphore_signal(barrier, inc=1, device_id=(device,), device_id_type=MESH)
    pl.semaphore_wait(barrier, 4)

    for j in range(CHUNKS):
        own_copy(j).wait()
        pair(0, j, me).start()
        for kind in range(3):
            link(kind, j, me, near[kind]).start()

    onward = ((5, 2), (3, 0), (4, 1))

    def serve_near(j):
        for kind in range(3):
            link(kind, j, near[kind], near[kind]).wait_recv()
            pair(1 + kind, j, near[kind]).start()
            new_kind, d = onward[kind]
            link(new_kind, j, near[kind], near[d]).start()

    def serve_diag(j):
        for kind in range(3):
            link(3 + kind, j, diag[kind], near[kind]).wait_recv()
            pair(4 + kind, j, diag[kind]).start()

    def send_far(p):
        far(p, carried[pieces[p][0]]).start()

    def add(j, lo, hi, sources, first):
        for r in range(lo, hi, SUB):
            rs = pl.ds(r, SUB)
            total = None if first else acc[j, rs, :]
            for device in sources:
                ks = chip_rows(device)
                term = dot(a_all[rs, ks], b_all[j, ks, :])
                total = term if total is None else total + term
            acc[j, rs, :] = total

    a_copy(0).wait()

    @pl.loop(0, CHUNKS)
    def _(j):
        pair(0, j, mate).wait_recv()
        add(j, 0, rows, (me,), True)

    serve_near(0)
    for i in range(1, 8):
        a_copy(i).wait()

    @pl.loop(0, 2 * CHUNKS)
    def _(s):
        j = lax.rem(s, CHUNKS)
        phase = lax.div(s, CHUNKS)
        sources = [n + phase * (d - n) for n, d in zip(near, diag)]
        for i in range(3):
            pair(1 + 3 * phase + i, j, flip(sources[i], 1)).wait_recv()
        add(j, 0, half, sources, False)

        @pl.when(s < CHUNKS - 1)
        def _():
            serve_near(s + 1)

        @pl.when((s >= CHUNKS - 1) & (s < 2 * CHUNKS - 1))
        def _():
            serve_diag(s - (CHUNKS - 1))

        for c in range(CHUNKS):
            @pl.when(s == CHUNKS - 1 + c)
            def _():
                for p in range(6):
                    if pieces[p][1] == c:
                        send_far(p)

        add(j, half, rows, sources, False)

    for p in range(6):
        far(p, dev_far).wait_recv()
        if p < 3:
            pair(7, p, dev_far).start()
    pair(7, 3, dev_far).start()
    for j in range(CHUNKS):
        pair(7, j, flip(dev_far, 1)).wait_recv()

    for j in range(CHUNKS):
        for kind in range(3):
            link(kind, j, me, near[kind]).wait_send()
            new_kind, d = onward[kind]
            link(new_kind, j, near[kind], near[d]).wait_send()
        for i in range(8):
            pair(i, j, order[i]).wait_send()
    for p in range(6):
        far(p, carried[pieces[p][0]]).wait_send()


def finish_kernel(b_ref, a_ref, acc_ref, c_ref):
    step = pl.program_id(0)
    steps = pl.num_programs(0)
    chunks, size, wide = b_ref.shape
    rows = c_ref.shape[0]
    far = 7 - lax.div(lax.axis_index("fsdp"), 2)
    ks = pl.ds(pl.multiple_of(far * 256, 256), 256)

    @pl.when(step < steps - 1)
    def _():
        for j in range(chunks):
            for r in range(0, rows, SUB):
                rs = pl.ds(pl.multiple_of(step * rows + r, SUB), SUB)
                total = acc_ref[j, rs, :] + dot(a_ref[rs, ks], b_ref[j, ks, :])
                c_ref[pl.ds(r, SUB), j * wide:(j + 1) * wide] = total.astype(c_ref.dtype)

    @pl.when(step == steps - 1)
    def _():
        base = a_ref.shape[0] - rows
        for j in range(chunks):
            for r in range(0, rows, SUB):
                total = dot(a_ref[pl.ds(base + r, SUB), :], b_ref[j])
                c_ref[pl.ds(r, SUB), j * wide:(j + 1) * wide] = total.astype(c_ref.dtype)


def solution(mesh):
    def local(a, b):
        rows, size = a.shape
        depth, cols = b.shape
        wide = cols // CHUNKS
        main = rows - LAST
        vmem = pl.BlockSpec(memory_space=pltpu.VMEM)
        hbm = pl.BlockSpec(memory_space=pl.ANY)
        dma = pltpu.SemaphoreType.DMA
        b_all, a_all, acc = pl.pallas_call(
            gather_kernel,
            out_shape=(
                pltpu.VMEM((CHUNKS, size, wide), jnp.bfloat16),
                pltpu.VMEM((rows, size), jnp.bfloat16),
                pltpu.VMEM((CHUNKS, main, wide), jnp.float32),
            ),
            in_specs=[hbm, hbm],
            out_specs=(vmem, vmem, vmem),
            scratch_shapes=[
                dma((8,)), dma((CHUNKS,)),
                dma((6, CHUNKS)), dma((6, CHUNKS)),
                dma((8, CHUNKS)), dma((8, CHUNKS)),
                dma((6,)), dma((6,)),
            ],
            compiler_params=pltpu.CompilerParams(collective_id=0, has_side_effects=True, vmem_limit_bytes=1 << 20),
            name="gather",
        )(a, pltpu.with_memory_space_constraint(b, pltpu.HBM))
        return pl.pallas_call(
            finish_kernel,
            grid=(rows // LAST,),
            out_shape=jax.ShapeDtypeStruct((rows, cols), jnp.bfloat16),
            in_specs=[vmem, vmem, vmem],
            out_specs=pl.BlockSpec((LAST, cols), lambda i: (i, 0)),
            compiler_params=pltpu.CompilerParams(vmem_limit_bytes=8 << 20),
            name="finish",
        )(*(pltpu.with_memory_space_constraint(v, pltpu.VMEM) for v in (b_all, a_all, acc)))

    spec = P("fsdp", None)
    return jax.shard_map(local, mesh=mesh, in_specs=(spec, spec), out_specs=spec, check_vma=False)
```

time: 110 us -> 54.4 us (0.49)
  waiting for transfers between devices: 54.5 us -> 0 us
  Pallas kernels: 0 us -> 54.2 us
  matrix products: 41.8 us -> 0 us
  between operations: 13.4 us -> 0.01 us
    pallas_call x0 -> x2, Pallas kernels: none -> 54.2 us  [the longest x1 41.4 us: local(): pl.pallas_call(gather_kernel, out_shape=(pltpu.VMEM((CHUNKS, size, wide),...]
    all_gather x1 -> x0, waiting for transfers between devices: 53.8 us -> none  [local_fn(): full_right = lax.all_gather(right_blk, 'fsdp', axis=0, tiled=True)]
    dot_general x1 -> x0, matrix products: 41.8 us -> none  [local_fn(): jnp.dot(left_blk, full_right, preferred_element_type=jnp.float32)]
  transfers between devices with their start and end apart: 1 -> 0, of which waited for: 1 -> 0; matrix products, arithmetic and copies ran while one was open for 0% -> 0% of each run, Pallas kernels for 0% -> 0%
where the time goes in v1:
time: 54.4 us; the launch traced here: 54.2 us
  Pallas kernels  54.2 us (100%)
    pallas_call x1, Pallas kernels, local(): pl.pallas_call(gather_kernel, out_shape=(pltpu.VMEM((CHUNKS, size, wide),...  41.4 us
    pallas_call x1, Pallas kernels, local(): pl.pallas_call(finish_kernel, grid=(rows // LAST,), out_shape=jax.ShapeDt...  12.8 us

profile of v1, /device:TPU:0, one launch (start us, length us, event | category | flops | bytes accessed | tf_op | source)
XLA Modules:
  0.0 54.2 jit_solution(11535963309886371398)
XLA Ops:
  0.0 41.4 %gather.1 = (bf16[4,2048,512]{2,1,0:T(8,128)(2,1)S(1)}, bf16[4096,2048]{1,0:T(8,128)(2,1)S(1)}, f32[4,3584,512]{2,1,0:T(8,128)S(1)}) custom-call(bf16[4096,2048]{1,0:T(8,128)(2,1)} %a_hbm.1, bf16[128,2048]{1,0:T(8,128)(2,1)} %b_hbm.1), custom_call_target="tpu_custom_call" | custom-call | tf_op jit(solution)/shard_map/gather/pallas_call | solution.py:202
  41.4 12.8 %finish.1 = bf16[4096,2048]{1,0:T(8,128)(2,1)} custom-call(bf16[4,2048,512]{2,1,0:T(8,128)(2,1)S(1)} %get-tuple-element.8.b_ref, bf16[4096,2048]{1,0:T(8,128)(2,1)S(1)} %get-tuple-element.9.a_ref, f32[4,3584,512]{2,1,0:T(8,128)S(1)} %get-tuple-element.10.acc_ref), custom_call_target="tpu_custom_call" | custom-call | tf_op jit(solution)/shard_map/finish/pallas_call | solution.py:220

commit v2 on v0

v2 whole, which is shorter than its diff:
```python
import jax
import jax.numpy as jnp
from jax import lax
from jax.experimental import pallas as pl
from jax.experimental.pallas import tpu as pltpu
from jax.sharding import PartitionSpec as P

MESH = pl.DeviceIdType.MESH
CHUNKS = 8
SUB = 256
LAST = 256
STAGE = 768
EARLY = 5


def flip(index, stride):
    return index + stride - 2 * stride * lax.rem(lax.div(index, stride), 2)


def dot(a, b):
    return jnp.dot(a, b, preferred_element_type=jnp.float32)


def pick(d, values):
    return jnp.where(d == 0, values[0], jnp.where(d == 1, values[1], values[2]))


def gather_kernel(a_hbm, b_hbm, b_all, a_all, acc, a_sem, own_sem, sent, near_sem, diag_sem, far_sem, pair_own, pair_near, pair_diag, pair_far):
    me = lax.axis_index("fsdp")
    depth = b_hbm.shape[0]
    wide = b_all.shape[2]
    rows = acc.shape[1]
    mate = flip(me, 1)
    dev_x, dev_y, dev_z = flip(me, 2), flip(me, 4), flip(me, 8)
    dev_xy, dev_yz, dev_zx = flip(dev_x, 4), flip(dev_y, 8), flip(dev_z, 2)
    dev_far = flip(dev_xy, 8)
    near = (dev_x, dev_y, dev_z)
    diag = (dev_xy, dev_yz, dev_zx)
    order = (me, *near, *diag, dev_far)
    split = CHUNKS - 2

    def chip_rows(device):
        return pl.ds(pl.multiple_of(lax.div(device, 2) * (2 * depth), 2 * depth), 2 * depth)

    def block(j, device, columns=slice(None)):
        return b_all.at[j, pl.ds(pl.multiple_of(device * depth, depth), depth), columns]

    def link(sem, j, device, target, columns=slice(None)):
        ref = block(j, device, columns)
        return pltpu.make_async_remote_copy(ref, ref, sent.at[0], sem, device_id=(target,), device_id_type=MESH)

    def pair(sem, j, device):
        ref = block(j, device)
        return pltpu.make_async_remote_copy(ref, ref, sent.at[1], sem, device_id=(mate,), device_id_type=MESH)

    def settle(sem, ref):
        pltpu.make_async_copy(ref, ref, sem).wait()

    shift = lax.rem(me, 2) * depth

    def three(j):
        return b_all.at[j, pl.ds(pl.multiple_of(shift, depth), 3 * depth), :]

    def across(lo, hi, device):
        return b_all.at[pl.ds(lo, hi - lo), pl.ds(pl.multiple_of(device * depth, depth), depth), :]

    def a_copy(i):
        cols = chip_rows(order[i])
        group = 0 if i == 0 else 1 if i < 4 else 2
        return pltpu.make_async_copy(a_hbm.at[:, cols], a_all.at[:, cols], a_sem.at[group])

    def a_wait(lo, hi):
        width = (hi - lo) * 2 * depth
        settle(a_sem.at[0 if lo == 0 else 1 if lo == 1 else 2], a_all.at[:, pl.ds(pl.multiple_of(shift, depth), width)])

    def own_copy(j):
        return pltpu.make_async_copy(b_hbm.at[:, pl.ds(j * wide, wide)], block(j, me), own_sem)

    for j in range(CHUNKS):
        own_copy(j).start()
    a_copy(0).start()

    barrier = pltpu.get_barrier_semaphore()
    for device in (mate, *near):
        pl.semaphore_signal(barrier, inc=1, device_id=(device,), device_id_type=MESH)
    pl.semaphore_wait(barrier, 4)

    settle(own_sem, across(0, CHUNKS, me))
    for j in range(CHUNKS):
        for kind in range(3):
            link(near_sem.at[j], j, me, near[kind]).start()
        pair(pair_own.at[0 if j < EARLY else 1], j, me).start()
    for i in range(1, 4):
        a_copy(i).start()

    def serve_near(j):
        settle(near_sem.at[j], three(j))
        for kind, d in enumerate((2, 0, 1)):
            pair(pair_near.at[j], j, near[kind]).start()
            link(diag_sem.at[j], j, near[kind], near[d]).start()

    half = wide // 2
    halves = (pl.ds(0, half), pl.ds(half, half))

    def send_far(j):
        if isinstance(j, int):
            if j == split:
                link(far_sem.at[1], j, dev_xy, dev_z, halves[0]).start()
                link(far_sem.at[1], j, dev_yz, dev_x, halves[1]).start()
                return
            d = min(j // 2, 2)
            source, target = (dev_xy, dev_yz, dev_zx)[d], (dev_z, dev_x, dev_y)[d]
        else:
            d = lax.div(j, 2)
            source, target = pick(d, (dev_xy, dev_yz, dev_zx)), pick(d, (dev_z, dev_x, dev_y))
        link(far_sem.at[0 if not isinstance(j, int) or j < split else 1], j, source, target).start()

    def serve_diag(j):
        settle(diag_sem.at[j], three(j))
        send_far(j)
        for kind in range(3):
            pair(pair_diag.at[j], j, diag[kind]).start()

    def serve_far(group):
        lo, hi = ((0, split), (split, CHUNKS))[group]
        settle(far_sem.at[group], across(lo, hi, dev_far))
        for j in range(lo, hi):
            pair(pair_far, j, dev_far).start()

    def add(j, sources, first=False):
        for r in range(0, rows, SUB):
            rs = pl.ds(r, SUB)
            total = None if first else acc[j, rs, :]
            for device in sources:
                ks = chip_rows(device)
                term = dot(a_all[rs, ks], b_all[j, ks, :])
                total = term if total is None else total + term
            acc[j, rs, :] = total

    a_wait(0, 1)
    settle(pair_own.at[0], across(0, EARLY, mate))
    for j in range(EARLY):
        add(j, (me,), True)
    serve_near(0)
    for i in range(4, 8):
        a_copy(i).start()
    settle(pair_own.at[1], across(EARLY, CHUNKS, mate))
    for j in range(EARLY, CHUNKS):
        add(j, (me,), True)

    def steps(phase, lo, hi, serve):
        @pl.loop(lo + phase * CHUNKS, hi + phase * CHUNKS)
        def _(s):
            j = lax.rem(s, CHUNKS)
            late = lax.div(s, CHUNKS)
            serve(j)
            sources = [n + late * (d - n) for n, d in zip(near, diag)]
            settle((pair_diag if phase else pair_near).at[j], three(j))
            add(j, sources)

    def plan(table):
        def serve(j):
            for k, parts in table.items():
                @pl.when(j == k)
                def _():
                    for part, arg in parts:
                        part(arg)
        return serve

    a_wait(1, 4)
    steps(0, 0, 6, lambda j: serve_near(j + 1))
    steps(0, 6, 8, plan({6: ((serve_near, 7), (serve_diag, 0)), 7: ((serve_diag, 1),)}))
    a_wait(4, 8)
    steps(1, 0, 2, plan({0: ((serve_diag, 2),), 1: ((serve_diag, 3), (serve_diag, 4))}))
    steps(1, 2, 4, plan({2: ((serve_diag, 5),), 3: ((serve_diag, 6),)}))
    steps(1, 4, 6, plan({4: ((serve_diag, 7),)}))
    steps(1, 6, 8, plan({6: ((serve_far, 0),), 7: ((serve_far, 1),)}))

    settle(pair_far, across(0, CHUNKS, flip(dev_far, 1)))
    settle(sent.at[0], b_all.at[pl.ds(0, CHUNKS - 1), pl.ds(0, 8 * depth), :])
    settle(sent.at[1], b_all.at[:, pl.ds(0, 8 * depth), :])


def finish_kernel(b_ref, a_ref, acc_ref, c_hbm, stage, sem):
    chunks, size, wide = b_ref.shape
    main = acc_ref.shape[1]
    blocks = main // STAGE
    last = c_hbm.shape[0] - main
    depth = size // 8
    far = 7 - lax.div(lax.axis_index("fsdp"), 2)
    ks = pl.ds(pl.multiple_of(far * depth, depth), depth)

    def put(i):
        rs = pl.ds(pl.multiple_of(i * STAGE, STAGE), STAGE)
        slot = lax.rem(i, 2)
        return pltpu.make_async_copy(stage.at[slot], c_hbm.at[rs, :], sem.at[slot])

    @pl.loop(0, blocks)
    def _(i):
        @pl.when(i >= 2)
        def _():
            put(i - 2).wait()

        slot = lax.rem(i, 2)
        for j in range(chunks):
            for r in range(0, STAGE, SUB):
                rs = pl.ds(pl.multiple_of(i * STAGE + r, SUB), SUB)
                total = acc_ref[j, rs, :] + dot(a_ref[rs, ks], b_ref[j, ks, :])
                stage[slot, pl.ds(r, SUB), j * wide:(j + 1) * wide] = total.astype(stage.dtype)
        put(i).start()

    put(blocks - 2).wait()
    slot = blocks % 2
    for j in range(chunks):
        for r in range(0, last, SUB):
            total = dot(a_ref[pl.ds(main + r, SUB), :], b_ref[j])
            stage[slot, pl.ds(r, SUB), j * wide:(j + 1) * wide] = total.astype(stage.dtype)
    tail = pltpu.make_async_copy(stage.at[slot, pl.ds(0, last)], c_hbm.at[pl.ds(main, last), :], sem.at[slot])
    tail.start()
    put(blocks - 1).wait()
    tail.wait()


def solution(mesh):
    def local(a, b):
        rows, size = a.shape
        depth, cols = b.shape
        wide = cols // CHUNKS
        main = rows - LAST
        vmem = pl.BlockSpec(memory_space=pltpu.VMEM)
        hbm = pl.BlockSpec(memory_space=pl.ANY)
        dma = pltpu.SemaphoreType.DMA
        parts = pl.pallas_call(
            gather_kernel,
            out_shape=(
                pltpu.VMEM((CHUNKS, size, wide), jnp.bfloat16),
                pltpu.VMEM((rows, size), jnp.bfloat16),
                pltpu.VMEM((CHUNKS, main, wide), jnp.float32),
            ),
            in_specs=[hbm, hbm],
            out_specs=(vmem, vmem, vmem),
            scratch_shapes=[
                dma((3,)), dma, dma((2,)),
                dma((CHUNKS,)), dma((CHUNKS,)), dma((2,)),
                dma((2,)), dma((CHUNKS,)), dma((CHUNKS,)), dma,
            ],
            compiler_params=pltpu.CompilerParams(collective_id=0, has_side_effects=True, vmem_limit_bytes=1 << 20),
            name="gather",
        )(a, pltpu.with_memory_space_constraint(b, pltpu.HBM))
        return pl.pallas_call(
            finish_kernel,
            out_shape=jax.ShapeDtypeStruct((rows, cols), jnp.bfloat16),
            in_specs=[vmem, vmem, vmem],
            out_specs=hbm,
            scratch_shapes=[pltpu.VMEM((2, STAGE, cols), jnp.bfloat16), dma((2,))],
            compiler_params=pltpu.CompilerParams(vmem_limit_bytes=7 << 20),
            name="finish",
        )(*(pltpu.with_memory_space_constraint(v, pltpu.VMEM) for v in parts))

    spec = P("fsdp", None)
    return jax.shard_map(local, mesh=mesh, in_specs=(spec, spec), out_specs=spec, check_vma=False)
```

time: 110 us -> 49.6 us (0.45)
  waiting for transfers between devices: 54.5 us -> 0 us
  Pallas kernels: 0 us -> 49.3 us
  matrix products: 41.8 us -> 0 us
  between operations: 13.4 us -> 0.17 us
    all_gather x1 -> x0, waiting for transfers between devices: 53.8 us -> none  [local_fn(): full_right = lax.all_gather(right_blk, 'fsdp', axis=0, tiled=True)]
    pallas_call x0 -> x2, Pallas kernels: none -> 49.3 us  [the longest x1 39.3 us: local(): pl.pallas_call(gather_kernel, out_shape=(pltpu.VMEM((CHUNKS, size, wide),...]
    dot_general x1 -> x0, matrix products: 41.8 us -> none  [local_fn(): jnp.dot(left_blk, full_right, preferred_element_type=jnp.float32)]
  transfers between devices with their start and end apart: 1 -> 0, of which waited for: 1 -> 0; matrix products, arithmetic and copies ran while one was open for 0% -> 0% of each run, Pallas kernels for 0% -> 0%
where the time goes in v2:
time: 49.6 us; the launch traced here: 49.5 us
  Pallas kernels  49.3 us (99%)
    pallas_call x1, Pallas kernels, local(): pl.pallas_call(gather_kernel, out_shape=(pltpu.VMEM((CHUNKS, size, wide),...  39.3 us
    pallas_call x1, Pallas kernels, local(): pl.pallas_call(finish_kernel, out_shape=jax.ShapeDtypeStruct((rows, cols)...  9.99 us

profile of v2, /device:TPU:0, one launch (start us, length us, event | category | flops | bytes accessed | tf_op | source)
XLA Modules:
  0.0 49.5 jit_solution(9427783130990777111)
XLA Ops:
  0.0 39.3 %gather.1 = (bf16[8,2048,256]{2,1,0:T(8,128)(2,1)S(1)}, bf16[4096,2048]{1,0:T(8,128)(2,1)S(1)}, f32[8,3840,256]{2,1,0:T(8,128)S(1)}) custom-call(bf16[4096,2048]{1,0:T(8,128)(2,1)} %a_hbm.1, bf16[128,2048]{1,0:T(8,128)(2,1)} %b_hbm.1), custom_call_target="tpu_custom_call" | custom-call | tf_op jit(solution)/shard_map/gather/pallas_call | solution.py:233
  39.3 10.0 %finish.1 = bf16[4096,2048]{1,0:T(8,128)(2,1)} custom-call(bf16[8,2048,256]{2,1,0:T(8,128)(2,1)S(1)} %get-tuple-element.8.b_ref, bf16[4096,2048]{1,0:T(8,128)(2,1)S(1)} %get-tuple-element.9.a_ref, f32[8,3840,256]{2,1,0:T(8,128)S(1)} %get-tuple-element.10.acc_ref), custom_call_target="tpu_custom_call" | custom-call | tf_op jit(solution)/shard_map/finish/pallas_call | solution.py:250

commit v3 on v2

v3 whole, which is shorter than its diff:
```python
import jax
import jax.numpy as jnp
from jax import lax
from jax.experimental import pallas as pl
from jax.experimental.pallas import tpu as pltpu
from jax.sharding import PartitionSpec as P

MESH = pl.DeviceIdType.MESH
CHUNKS = 8
SUB = 512
TILE = 256
SLOTS = 4
LEFT = 2
EARLY = 5


def flip(index, stride):
    return index + stride - 2 * stride * lax.rem(lax.div(index, stride), 2)


def dot(a, b):
    return jnp.dot(a, b, preferred_element_type=jnp.float32)


UNITS = 2
RING = 4
LAG = 2


def accumulators():
    return [pltpu.ACC(q)((TILE, TILE), jnp.float32) for q in range(UNITS) for _ in range(RING)]


def stage_right(right, n):
    for q in range(UNITS):
        pltpu.matmul_push_rhs(right(n, q), staging_register=n % 2, mxu_index=q)


def result(tiles, i, q):
    return pltpu.matmul_pop(tiles[q * RING + i % RING])


def pick(d, values):
    return jnp.where(d == 0, values[0], jnp.where(d == 1, values[1], values[2]))


def gather_kernel(a_hbm, b_hbm, b_all, a_all, acc, a_sem, own_sem, sent, near_sem, diag_sem, far_sem, pair_own, pair_near, pair_diag, pair_far):
    me = lax.axis_index("fsdp")
    depth = b_hbm.shape[0]
    wide = b_all.shape[2]
    rows = acc.shape[1]
    mate = flip(me, 1)
    dev_x, dev_y, dev_z = flip(me, 2), flip(me, 4), flip(me, 8)
    dev_xy, dev_yz, dev_zx = flip(dev_x, 4), flip(dev_y, 8), flip(dev_z, 2)
    dev_far = flip(dev_xy, 8)
    near = (dev_x, dev_y, dev_z)
    diag = (dev_xy, dev_yz, dev_zx)
    order = (me, *near, *diag, dev_far)

    def chip_rows(device):
        return pl.ds(pl.multiple_of(lax.div(device, 2) * (2 * depth), 2 * depth), 2 * depth)

    def block(j, device, start=0, count=None):
        return b_all.at[j, pl.ds(pl.multiple_of(device * depth + start, 16), count or depth), :]

    def link(sem, j, device, target, start=0, count=None):
        ref = block(j, device, start, count)
        return pltpu.make_async_remote_copy(ref, ref, sent.at[0], sem, device_id=(target,), device_id_type=MESH)

    def pair(sem, j, device):
        ref = block(j, device)
        return pltpu.make_async_remote_copy(ref, ref, sent.at[1], sem, device_id=(mate,), device_id_type=MESH)

    def settle(sem, ref):
        pltpu.make_async_copy(ref, ref, sem).wait()

    shift = lax.rem(me, 2) * depth

    def three(j):
        return b_all.at[j, pl.ds(pl.multiple_of(shift, depth), 3 * depth), :]

    def across(lo, hi, device):
        return b_all.at[pl.ds(lo, hi - lo), pl.ds(pl.multiple_of(device * depth, depth), depth), :]

    def a_copy(i):
        cols = chip_rows(order[i])
        group = 0 if i == 0 else 1 if i < 4 else 2
        return pltpu.make_async_copy(a_hbm.at[:, cols], a_all.at[:, cols], a_sem.at[group])

    def a_wait(lo, hi):
        width = (hi - lo) * 2 * depth
        settle(a_sem.at[0 if lo == 0 else 1 if lo == 1 else 2], a_all.at[:, pl.ds(pl.multiple_of(shift, depth), width)])

    def own_copy(j):
        return pltpu.make_async_copy(b_hbm.at[:, pl.ds(j * wide, wide)], block(j, me), own_sem)

    for j in range(CHUNKS):
        own_copy(j).start()
    a_copy(0).start()

    barrier = pltpu.get_barrier_semaphore()
    for device in (mate, *near):
        pl.semaphore_signal(barrier, inc=1, device_id=(device,), device_id_type=MESH)
    pl.semaphore_wait(barrier, 4)

    settle(own_sem, across(0, CHUNKS, me))
    for j in range(CHUNKS):
        for kind in range(3):
            link(near_sem.at[j], j, me, near[kind]).start()
        pair(pair_own.at[0 if j < EARLY else 1], j, me).start()
    for i in range(1, 4):
        a_copy(i).start()

    def serve_near(j):
        settle(near_sem.at[j], three(j))
        for kind, d in enumerate((2, 0, 1)):
            pair(pair_near.at[j], j, near[kind]).start()
            link(diag_sem.at[j], j, near[kind], near[d]).start()

    part_rows = ((48, 48, 32), (32, 48, 48), (48, 32, 48))

    def send_far(j):
        start = 0
        for d, count in enumerate(part_rows[j % 3]):
            source, target = ((dev_xy, dev_z), (dev_yz, dev_x), (dev_zx, dev_y))[d]
            link(far_sem, j, source, target, start, count).start()
            start += count

    def serve_diag(j):
        settle(diag_sem.at[j], three(j))
        send_far(j)
        for kind in range(3):
            pair(pair_diag.at[j], j, diag[kind]).start()

    def serve_far():
        settle(far_sem, across(0, CHUNKS, dev_far))
        for j in range(CHUNKS):
            pair(pair_far, j, dev_far).start()

    def add(j, sources, first=False, count=1):
        for r in range(0, rows, SUB):
            rs = pl.ds(r, SUB)
            for c in range(count):
                total = None if first else acc[j + c, rs, :]
                for device in sources:
                    ks = chip_rows(device)
                    term = dot(a_all[rs, ks], b_all[j + c, ks, :])
                    total = term if total is None else total + term
                acc[j + c, rs, :] = total

    a_wait(0, 1)
    settle(pair_own.at[0], across(0, EARLY, mate))
    for j in range(EARLY):
        add(j, (me,), True)
    serve_near(0)
    for i in range(4, 8):
        a_copy(i).start()
    settle(pair_own.at[1], across(EARLY, CHUNKS, mate))
    for j in range(EARLY, CHUNKS):
        add(j, (me,), True)

    def steps(phase, lo, hi, serve, count=1):
        @pl.loop(0, (hi - lo) // count)
        def _(s):
            j = lo + s * count
            late = lax.div(j + phase * CHUNKS, CHUNKS)
            serve(j)
            sources = [n + late * (d - n) for n, d in zip(near, diag)]
            for c in range(count):
                settle((pair_diag if phase else pair_near).at[j + c], three(j + c))
            add(j, sources, False, count)

    def plan(table):
        def serve(j):
            for k, parts in table.items():
                @pl.when(j == k)
                def _():
                    for part, arg in parts:
                        part(arg)
        return serve

    a_wait(1, 4)
    steps(0, 0, 4, plan({0: ((serve_near, 1),), 1: ((serve_near, 2),), 2: ((serve_near, 3),), 3: ((serve_near, 4), (serve_near, 5))}))
    steps(0, 4, 6, plan({4: ((serve_near, 6),)}), 2)
    steps(0, 6, 8, plan({6: ((serve_near, 7), (serve_diag, 0)), 7: ((serve_diag, 1), (serve_diag, 2))}))
    a_wait(4, 8)
    steps(1, 0, 2, plan({0: ((serve_diag, 3),)}), 2)
    steps(1, 2, 3, plan({2: ((serve_diag, 4), (serve_diag, 5))}))
    steps(1, 3, 5, plan({3: ((serve_diag, 6), (serve_diag, 7))}), 2)
    steps(1, 5, 6, lambda j: serve_far())

    for j in range(CHUNKS - LEFT, CHUNKS):
        settle(pair_diag.at[j], three(j))
    settle(pair_far, across(0, CHUNKS, flip(dev_far, 1)))
    settle(sent.at[0], b_all.at[pl.ds(0, CHUNKS - 1), pl.ds(0, 8 * depth), :])
    settle(sent.at[1], b_all.at[:, pl.ds(0, 8 * depth), :])


def finish_kernel(*refs):
    pl.run_scoped(lambda *tiles: finish_body(tiles, *refs), *accumulators())


def finish_body(tiles, b_ref, a_ref, acc_ref, c_hbm, stage, sem):
    chunks, size, wide = b_ref.shape
    blocks = c_hbm.shape[0] // TILE
    count = chunks // UNITS
    depth = size // 8
    chip = lax.div(lax.axis_index("fsdp"), 2)
    far = 7 - chip
    chips = (far, flip(far, 1), flip(far, 2), flip(far, 4))

    def part(device):
        return pl.ds(pl.multiple_of(device * depth, depth), depth)

    def rows_of(b):
        return pl.ds(pl.multiple_of(b * TILE, TILE), TILE)

    def put(b):
        slot = lax.rem(b, SLOTS)
        return pltpu.make_async_copy(stage.at[slot], c_hbm.at[rows_of(b), :], sem.at[slot])

    def keep(b, slot, i):
        for q in range(UNITS):
            j = UNITS * i + q
            total = acc_ref[j, rows_of(b), :] + result(tiles, i, q)
            stage[slot, :, j * wide:(j + 1) * wide] = total.astype(stage.dtype)

    passes = [(i, d) for i in range(count) for d in chips[:1 if UNITS * i < chunks - LEFT else 4]]

    def right(n, q):
        i, d = passes[n]
        return b_ref[UNITS * i + q, part(d), :]

    stage_right(right, 0)

    def work(b, start=True, wait=True):
        before = b - 1 if start else 0
        for n, (i, d) in enumerate(passes):
            if n + 1 < len(passes):
                stage_right(right, n + 1)
            for q in range(UNITS):
                pltpu.matmul_acc_lhs(tiles[q * RING + i % RING], a_ref[rows_of(b), part(d)], load_staged_rhs=n % 2)
            if n + 1 == len(passes):
                stage_right(right, 0)
            elif passes[n + 1][0] == i:
                continue
            if i < LAG:
                keep(before, lax.rem(b + SLOTS - 1, SLOTS), count - LAG + i)
            else:
                keep(b, lax.rem(b, SLOTS), i - LAG)
            if i == LAG - 1:
                if start:
                    put(b - 1).start()
                if wait:
                    put(b - SLOTS).wait()

    work(0, False, False)
    pl.loop(1, SLOTS)(lambda b: work(b, True, False))
    pl.loop(SLOTS, blocks)(work)
    for i in range(count - LAG, count):
        keep(blocks - 1, (blocks - 1) % SLOTS, i)
    put(blocks - 1).start()
    for q in range(UNITS):
        pltpu.matmul_acc_lhs(tiles[q * RING], a_ref[rows_of(0), part(far)], load_staged_rhs=0)
        result(tiles, 0, q)
    for b in range(blocks - SLOTS, blocks):
        put(b).wait()


def solution(mesh):
    def local(a, b):
        rows, size = a.shape
        depth, cols = b.shape
        wide = cols // CHUNKS
        vmem = pl.BlockSpec(memory_space=pltpu.VMEM)
        hbm = pl.BlockSpec(memory_space=pl.ANY)
        dma = pltpu.SemaphoreType.DMA
        parts = pl.pallas_call(
            gather_kernel,
            out_shape=(
                pltpu.VMEM((CHUNKS, size, wide), jnp.bfloat16),
                pltpu.VMEM((rows, size), jnp.bfloat16),
                pltpu.VMEM((CHUNKS, rows, wide), jnp.float32),
            ),
            in_specs=[hbm, hbm],
            out_specs=(vmem, vmem, vmem),
            scratch_shapes=[
                dma((3,)), dma, dma((2,)),
                dma((CHUNKS,)), dma((CHUNKS,)), dma,
                dma((2,)), dma((CHUNKS,)), dma((CHUNKS,)), dma,
            ],
            compiler_params=pltpu.CompilerParams(collective_id=0, has_side_effects=True, vmem_limit_bytes=7 << 20),
            name="gather",
        )(a, pltpu.with_memory_space_constraint(b, pltpu.HBM))
        return pl.pallas_call(
            finish_kernel,
            out_shape=jax.ShapeDtypeStruct((rows, cols), jnp.bfloat16),
            in_specs=[vmem, vmem, vmem],
            out_specs=hbm,
            scratch_shapes=[pltpu.VMEM((SLOTS, TILE, cols), jnp.bfloat16), dma((SLOTS,))],
            compiler_params=pltpu.CompilerParams(vmem_limit_bytes=7 << 20),
            name="finish",
        )(*(pltpu.with_memory_space_constraint(v, pltpu.VMEM) for v in parts))

    spec = P("fsdp", None)
    return jax.shard_map(local, mesh=mesh, in_specs=(spec, spec), out_specs=spec, check_vma=False)
```

time: 49.6 us -> 46.6 us (0.940)
  Pallas kernels: 49.3 us -> 46.3 us
    pallas_call x1, Pallas kernels: 39.3 us -> 35.8 us  [local(): pl.pallas_call(gather_kernel, out_shape=(pltpu.VMEM((CHUNKS, size, wide),...]
    pallas_call x1, Pallas kernels: 9.99 us -> 10.5 us  [local(): pl.pallas_call(finish_kernel, out_shape=jax.ShapeDtypeStruct((rows, cols)...]
where the time goes in v3:
time: 46.6 us; the launch traced here: 46.5 us
  Pallas kernels  46.3 us (99%)
    pallas_call x1, Pallas kernels, local(): pl.pallas_call(gather_kernel, out_shape=(pltpu.VMEM((CHUNKS, size, wide),...  35.8 us
    pallas_call x1, Pallas kernels, local(): pl.pallas_call(finish_kernel, out_shape=jax.ShapeDtypeStruct((rows, cols)...  10.5 us

profile of v3, /device:TPU:0, one launch (start us, length us, event | category | flops | bytes accessed | tf_op | source)
XLA Modules:
  0.0 46.5 jit_solution(12548775726371828906)
XLA Ops:
  0.0 35.8 %gather.1 = (bf16[8,2048,256]{2,1,0:T(8,128)(2,1)S(1)}, bf16[4096,2048]{1,0:T(8,128)(2,1)S(1)}, f32[8,4096,256]{2,1,0:T(8,128)S(1)}) custom-call(bf16[4096,2048]{1,0:T(8,128)(2,1)} %a_hbm.1, bf16[128,2048]{1,0:T(8,128)(2,1)} %b_hbm.1), custom_call_target="tpu_custom_call" | custom-call | tf_op jit(solution)/shard_map/gather/pallas_call | solution.py:278
  35.8 10.5 %finish.1 = bf16[4096,2048]{1,0:T(8,128)(2,1)} custom-call(bf16[8,2048,256]{2,1,0:T(8,128)(2,1)S(1)} %get-tuple-element.8.refs_0_, bf16[4096,2048]{1,0:T(8,128)(2,1)S(1)} %get-tuple-element.9.refs_1_, f32[8,4096,256]{2,1,0:T(8,128)S(1)} %get-tuple-element.10.refs_2_), custom_call_target="tpu_custom_call" | custom-call | tf_op jit(solution)/shard_map/finish/pallas_call | solution.py:295

commit v4 on v3

v4 whole, which is shorter than its diff:
```python
import jax
import jax.numpy as jnp
from jax import lax
from jax.experimental import pallas as pl
from jax.experimental.pallas import tpu as pltpu
from jax.sharding import PartitionSpec as P

MESH = pl.DeviceIdType.MESH
CHUNKS = 8
SUB = 1024
TILE = 256
BLOCK = 512
SLOTS = 3
LEFT = 2
EARLY = 5
NEAR = ((0, 1), (1, 1), (2, 1), (3, 1), (4, 2), (6, 2))


def flip(index, stride):
    return index + stride - 2 * stride * lax.rem(lax.div(index, stride), 2)


def dot(a, b):
    return jnp.dot(a, b, preferred_element_type=jnp.float32)


UNITS = 2
RING = 4
LAG = 2


def accumulators():
    return [pltpu.ACC(q)((TILE, TILE), jnp.float32) for q in range(UNITS) for _ in range(RING)]


def stage_right(right, n):
    for q in range(UNITS):
        pltpu.matmul_push_rhs(right(n, q), staging_register=n % 2, mxu_index=q)


def result(tiles, i, q):
    return pltpu.matmul_pop(tiles[q * RING + i % RING])


def pick(d, values):
    return jnp.where(d == 0, values[0], jnp.where(d == 1, values[1], values[2]))


def gather_kernel(a_hbm, b_hbm, b_all, a_all, acc, a_sem, own_sem, sent, near_sem, diag_sem, far_sem, pair_own, pair_near, pair_diag, pair_far):
    me = lax.axis_index("fsdp")
    depth = b_hbm.shape[0]
    wide = b_all.shape[2]
    rows = acc.shape[1]
    mate = flip(me, 1)
    dev_x, dev_y, dev_z = flip(me, 2), flip(me, 4), flip(me, 8)
    dev_xy, dev_yz, dev_zx = flip(dev_x, 4), flip(dev_y, 8), flip(dev_z, 2)
    dev_far = flip(dev_xy, 8)
    near = (dev_x, dev_y, dev_z)
    diag = (dev_xy, dev_yz, dev_zx)
    order = (me, *near, *diag, dev_far)

    def chip_rows(device):
        return pl.ds(pl.multiple_of(lax.div(device, 2) * (2 * depth), 2 * depth), 2 * depth)

    def block(j, device, n=1, start=0, count=None):
        return b_all.at[pl.ds(j, n), pl.ds(pl.multiple_of(device * depth + start, 16), count or depth), :]

    def link(sem, ref, target):
        return pltpu.make_async_remote_copy(ref, ref, sent.at[0], sem, device_id=(target,), device_id_type=MESH)

    def pair(sem, ref):
        return pltpu.make_async_remote_copy(ref, ref, sent.at[1], sem, device_id=(mate,), device_id_type=MESH)

    def settle(sem, ref):
        pltpu.make_async_copy(ref, ref, sem).wait()

    shift = lax.rem(me, 2) * depth

    def three(j, n=1):
        return b_all.at[pl.ds(j, n), pl.ds(pl.multiple_of(shift, depth), 3 * depth), :]

    def across(lo, hi, device):
        return b_all.at[pl.ds(lo, hi - lo), pl.ds(pl.multiple_of(device * depth, depth), depth), :]

    def a_copy(i):
        cols = chip_rows(order[i])
        group = 0 if i == 0 else 1 if i < 4 else 2
        return pltpu.make_async_copy(a_hbm.at[:, cols], a_all.at[:, cols], a_sem.at[group])

    def a_wait(lo, hi):
        width = (hi - lo) * 2 * depth
        settle(a_sem.at[0 if lo == 0 else 1 if lo == 1 else 2], a_all.at[:, pl.ds(pl.multiple_of(shift, depth), width)])

    def own_copy(j):
        return pltpu.make_async_copy(b_hbm.at[:, pl.ds(j * wide, wide)], b_all.at[j, pl.ds(pl.multiple_of(me * depth, depth), depth), :], own_sem)

    for j in range(CHUNKS):
        own_copy(j).start()
    a_copy(0).start()

    barrier = pltpu.get_barrier_semaphore()
    for device in (mate, *near):
        pl.semaphore_signal(barrier, inc=1, device_id=(device,), device_id_type=MESH)
    pl.semaphore_wait(barrier, 4)

    settle(own_sem, across(0, CHUNKS, me))
    for group, (lo, hi) in enumerate(((0, EARLY), (EARLY, CHUNKS))):
        pair(pair_own.at[group], across(lo, hi, me)).start()
    for u, (j, n) in enumerate(NEAR):
        for kind in range(3):
            link(near_sem.at[u], block(j, me, n), near[kind]).start()
    for i in range(1, 4):
        a_copy(i).start()

    def serve_near(u):
        j, n = NEAR[u]
        settle(near_sem.at[u], three(j, n))
        for kind, d in enumerate((2, 0, 1)):
            link(diag_sem.at[j // 2], block(j, near[kind], n), near[d]).start()
        for kind in range(3):
            pair(pair_near.at[u], block(j, near[kind], n)).start()

    part_rows = ((48, 48, 32), (32, 48, 48), (48, 32, 48))

    def serve_diag(u):
        settle(diag_sem.at[u], three(2 * u, 2))
        start = 0
        for d, count in enumerate(part_rows[u % 3]):
            source, target = ((dev_xy, dev_z), (dev_yz, dev_x), (dev_zx, dev_y))[d]
            link(far_sem, block(2 * u, source, 2, start, count), target).start()
            start += count
        for kind in range(3):
            pair(pair_diag.at[u], block(2 * u, diag[kind], 2)).start()

    def serve_far():
        settle(far_sem, across(0, CHUNKS, dev_far))
        pair(pair_far, across(0, CHUNKS, dev_far)).start()

    def add(j, sources, first=False, count=1):
        for r in range(0, rows, SUB):
            rs = pl.ds(r, SUB)
            for c in range(count):
                total = None if first else acc[j + c, rs, :]
                for device in sources:
                    ks = chip_rows(device)
                    term = dot(a_all[rs, ks], b_all[j + c, ks, :])
                    total = term if total is None else total + term
                acc[j + c, rs, :] = total

    a_wait(0, 1)
    settle(pair_own.at[0], across(0, EARLY, mate))
    for j in range(EARLY):
        add(j, (me,), True)
    serve_near(0)
    for i in range(4, 8):
        a_copy(i).start()
    settle(pair_own.at[1], across(EARLY, CHUNKS, mate))
    for j in range(EARLY, CHUNKS):
        add(j, (me,), True)

    def got_near(u):
        settle(pair_near.at[u], three(*NEAR[u]))

    def got_diag(u):
        settle(pair_diag.at[u], three(2 * u, 2))

    def steps(phase, lo, hi, table, count=1):
        @pl.loop(0, (hi - lo) // count)
        def _(s):
            j = lo + s * count
            late = lax.div(j + phase * CHUNKS, CHUNKS)
            for k, parts in table.items():
                @pl.when(j == k)
                def _():
                    for part, *arg in parts:
                        part(*arg)
            add(j, [n + late * (d - n) for n, d in zip(near, diag)], False, count)

    a_wait(1, 4)
    steps(0, 0, 4, {0: ((serve_near, 1), (got_near, 0)), 1: ((serve_near, 2), (got_near, 1)), 2: ((serve_near, 3), (got_near, 2)), 3: ((serve_near, 4), (got_near, 3))})
    steps(0, 4, 6, {4: ((got_near, 4),), 5: ((serve_near, 5),)})
    steps(0, 6, 8, {6: ((serve_diag, 0), (got_near, 5))}, 2)
    a_wait(4, 8)
    steps(1, 0, 2, {0: ((serve_diag, 1), (got_diag, 0))}, 2)
    steps(1, 2, 3, {2: ((serve_diag, 2), (got_diag, 1))})
    steps(1, 3, 5, {3: ((serve_diag, 3), (got_diag, 2))}, 2)
    steps(1, 5, 6, {5: ((serve_far,),)})
    got_diag(3)
    settle(pair_far, across(0, CHUNKS, flip(dev_far, 1)))
    settle(sent.at[0], b_all.at[pl.ds(0, CHUNKS - 1), pl.ds(0, 8 * depth), :])
    settle(sent.at[1], b_all.at[:, pl.ds(0, 8 * depth), :])


def finish_kernel(*refs):
    pl.run_scoped(lambda *tiles: finish_body(tiles, *refs), *accumulators())


def finish_body(tiles, b_ref, a_ref, acc_ref, c_hbm, stage, sem):
    chunks, size, wide = b_ref.shape
    blocks = c_hbm.shape[0] // BLOCK
    count = chunks // UNITS
    depth = size // 8
    chip = lax.div(lax.axis_index("fsdp"), 2)
    far = 7 - chip
    chips = (far, flip(far, 1), flip(far, 2), flip(far, 4))

    def part(device):
        return pl.ds(pl.multiple_of(device * depth, depth), depth)

    halves = BLOCK // TILE

    def rows_of(b, h=0, size=TILE):
        return pl.ds(pl.multiple_of(b * BLOCK + h * TILE, TILE), size)

    def put(b):
        slot = lax.rem(b, SLOTS)
        return pltpu.make_async_copy(stage.at[slot], c_hbm.at[rows_of(b, 0, BLOCK), :], sem.at[slot])

    def put_half(b, h):
        source = stage.at[b % SLOTS, pl.ds(h * TILE, TILE), :]
        return pltpu.make_async_copy(source, c_hbm.at[rows_of(b, h), :], sem.at[b % SLOTS if h == 0 else SLOTS])

    def keep(b, slot, t):
        h, i = divmod(t, count)
        for q in range(UNITS):
            j = UNITS * i + q
            total = acc_ref[j, rows_of(b, h), :] + result(tiles, t, q)
            stage[slot, pl.ds(h * TILE, TILE), j * wide:(j + 1) * wide] = total.astype(stage.dtype)

    passes = [(h * count + i, d) for h in range(halves) for i in range(count) for d in chips[:1 if UNITS * i < chunks - LEFT else 4]]
    every = halves * count

    def right(n, q):
        t, d = passes[n]
        return b_ref[UNITS * (t % count) + q, part(d), :]

    stage_right(right, 0)

    def work(b, start=True, wait=True, final=False):
        before = b - 1 if start else 0
        for n, (t, d) in enumerate(passes):
            if n + 1 < len(passes):
                stage_right(right, n + 1)
            for q in range(UNITS):
                pltpu.matmul_acc_lhs(tiles[q * RING + t % RING], a_ref[rows_of(b, t // count), part(d)], load_staged_rhs=n % 2)
            if n + 1 == len(passes):
                if not final:
                    stage_right(right, 0)
            elif passes[n + 1][0] == t:
                continue
            if t < LAG:
                keep(before, lax.rem(b + SLOTS - 1, SLOTS), every - LAG + t)
            else:
                keep(b, lax.rem(b, SLOTS), t - LAG)
            if t == LAG - 1:
                if start:
                    put(b - 1).start()
                if wait:
                    put(b - SLOTS).wait()
            if final and t == count + LAG - 1:
                put_half(b, 0).start()

    last = blocks - 1
    work(0, False, False)
    pl.loop(1, SLOTS)(lambda b: work(b, True, False))
    pl.loop(SLOTS, last)(work)
    work(last, True, True, True)
    for t in range(every - LAG, every):
        keep(last, last % SLOTS, t)
    put_half(last, 1).start()
    for b in range(blocks - SLOTS, last):
        put(b).wait()
    for h in range(halves):
        put_half(last, h).wait()


def solution(mesh):
    def local(a, b):
        rows, size = a.shape
        depth, cols = b.shape
        wide = cols // CHUNKS
        vmem = pl.BlockSpec(memory_space=pltpu.VMEM)
        hbm = pl.BlockSpec(memory_space=pl.ANY)
        dma = pltpu.SemaphoreType.DMA
        parts = pl.pallas_call(
            gather_kernel,
            out_shape=(
                pltpu.VMEM((CHUNKS, size, wide), jnp.bfloat16),
                pltpu.VMEM((rows, size), jnp.bfloat16),
                pltpu.VMEM((CHUNKS, rows, wide), jnp.float32),
            ),
            in_specs=[hbm, hbm],
            out_specs=(vmem, vmem, vmem),
            scratch_shapes=[
                dma((3,)), dma, dma((2,)),
                dma((len(NEAR),)), dma((CHUNKS // 2,)), dma,
                dma((2,)), dma((len(NEAR),)), dma((CHUNKS // 2,)), dma,
            ],
            compiler_params=pltpu.CompilerParams(collective_id=0, has_side_effects=True, vmem_limit_bytes=7 << 20),
            name="gather",
        )(a, pltpu.with_memory_space_constraint(b, pltpu.HBM))
        return pl.pallas_call(
            finish_kernel,
            out_shape=jax.ShapeDtypeStruct((rows, cols), jnp.bfloat16),
            in_specs=[vmem, vmem, vmem],
            out_specs=hbm,
            scratch_shapes=[pltpu.VMEM((SLOTS, BLOCK, cols), jnp.bfloat16), dma((SLOTS + 1,))],
            compiler_params=pltpu.CompilerParams(vmem_limit_bytes=15 << 19),
            name="finish",
        )(*(pltpu.with_memory_space_constraint(v, pltpu.VMEM) for v in parts))

    spec = P("fsdp", None)
    return jax.shard_map(local, mesh=mesh, in_specs=(spec, spec), out_specs=spec, check_vma=False)
```

time: 46.6 us -> 45.6 us (0.979)
  Pallas kernels: 46.3 us -> 45.3 us
    pallas_call x1, Pallas kernels: 10.5 us -> 9.93 us  [local(): pl.pallas_call(finish_kernel, out_shape=jax.ShapeDtypeStruct((rows, cols)...]
where the time goes in v4:
time: 45.6 us; the launch traced here: 45.4 us
  Pallas kernels  45.3 us (99%)
    pallas_call x1, Pallas kernels, local(): pl.pallas_call(gather_kernel, out_shape=(pltpu.VMEM((CHUNKS, size, wide),...  35.4 us
    pallas_call x1, Pallas kernels, local(): pl.pallas_call(finish_kernel, out_shape=jax.ShapeDtypeStruct((rows, cols)...  9.93 us

profile of v4, /device:TPU:0, one launch (start us, length us, event | category | flops | bytes accessed | tf_op | source)
XLA Modules:
  0.0 45.4 jit_solution(12151631524540703911)
XLA Ops:
  0.0 35.4 %gather.1 = (bf16[8,2048,256]{2,1,0:T(8,128)(2,1)S(1)}, bf16[4096,2048]{1,0:T(8,128)(2,1)S(1)}, f32[8,4096,256]{2,1,0:T(8,128)S(1)}) custom-call(bf16[4096,2048]{1,0:T(8,128)(2,1)} %a_hbm.1, bf16[128,2048]{1,0:T(8,128)(2,1)} %b_hbm.1), custom_call_target="tpu_custom_call" | custom-call | tf_op jit(solution)/shard_map/gather/pallas_call | solution.py:285
  35.4 9.9 %finish.1 = bf16[4096,2048]{1,0:T(8,128)(2,1)} custom-call(bf16[8,2048,256]{2,1,0:T(8,128)(2,1)S(1)} %get-tuple-element.8.refs_0_, bf16[4096,2048]{1,0:T(8,128)(2,1)S(1)} %get-tuple-element.9.refs_1_, f32[8,4096,256]{2,1,0:T(8,128)S(1)} %get-tuple-element.10.refs_2_), custom_call_target="tpu_custom_call" | custom-call | tf_op jit(solution)/shard_map/finish/pallas_call | solution.py:302
